TPU v7x, 256 devices: a whole 4x4x8 slice. The times are simulated.
256 devices in a mesh: dp: 2 (over core), seq: 16 (over z, x_lo), mp: 8 (over x_hi, y).
Axes of the slice: x: 4 (x_hi: 2, x_lo: 2; x = x_hi * 2 + x_lo), y: 4, z: 8, core: 2. Of those that a mesh axis runs over, the one named last changes fastest.
Arguments:
- queries: bfloat16 [4, 2048, 4096], P('dp', 'seq', 'mp'), may hold values from -6 to 6
- vision: bfloat16 [4, 1280, 4096], P('dp', 'seq'), may hold values from -6 to 6
- key_weight: bfloat16 [4096, 1024], P(None, 'mp'), may hold values from -0.09375 to 0.09375
- value_weight: bfloat16 [4096, 1024], P(None, 'mp'), may hold values from -0.09375 to 0.09375
- query_gain: float32 [128], replicated, may hold values from 0.6 to 6
- key_gain: float32 [128], replicated, may hold values from 0.6 to 6
- out_grad: bfloat16 [4, 2048, 4096], P('dp', 'seq', 'mp'), may hold values from -6 to 6
- tile_count: int32 [4], P('dp'), may hold values from 1 to 4, as said below
Outputs:
- query_grad: bfloat16 [4, 2048, 4096], P('dp', 'seq', 'mp')
- vision_grad: bfloat16 [4, 1280, 4096], P('dp', 'seq', 'mp')
- key_weight_grad: float32 [4096, 1024], P(None, 'mp')
- value_weight_grad: float32 [4096, 1024], P(None, 'mp')
Inputs may be any that keep to these rules, and one draw needn't show every extreme that they name: The live vision tokens of sample s are its first tile_count[s] * 320; some sample has 4 tiles and some other sample has 1.
All inputs are finite; a program needn't handle non-finite values.
Results may differ from a plain program's by a relative error of at most 0.03.
The roundings to bfloat16 on the way count: a program that leaves them out, or rounds other values in their place, can miss the bound.
Values may be sent and summed in bfloat16 or wider, within the bound.
A program may use at most 64 MiB of HBM per device.

v0:
```python
import jax
import jax.numpy as jnp
from jax import lax
from jax.sharding import PartitionSpec as P

MAX_TILES = 4


EPS = 1e-05
NEG = -1e30


def in_one_piece(arrays, axis, dim, along):
    ends, at = ([], 0)
    for a in arrays[:-1]:
        at += a.shape[along]
        ends.append(at)
    both = jnp.concatenate(arrays, axis=along)
    return tuple(jnp.split(lax.all_gather(both, axis, axis=dim, tiled=True), ends, axis=along))


def cut_along(x, dim, length):
    before, after = (x.shape[:dim], x.shape[dim + 1 :])
    return jnp.moveaxis(x.reshape(*before, length, -1, *after), dim, 0)


def sum_at_owner(x, axis, dim):
    length = lax.axis_size(axis)
    pieces = lax.all_to_all(cut_along(x, dim, length), axis, 0, 0, tiled=True)
    return jnp.sum(pieces.astype(jnp.float32), axis=0)


def in_one_piece_2(arrays, axis, dim, along):
    both = jnp.concatenate(arrays, axis=along)
    out, at, finished = (sum_at_owner(both, axis, dim), 0, [])
    for a in arrays:
        finished.append(lax.slice_in_dim(out, at, at + a.shape[along], axis=along))
        at += a.shape[along]
    return tuple(finished)


def in_one_piece_3(arrays, axis, dim, along):
    both = jnp.concatenate(arrays, axis=along)
    out, at, finished = (lax.psum_scatter(both, axis, scatter_dimension=dim, tiled=True), 0, [])
    for a in arrays:
        finished.append(lax.slice_in_dim(out, at, at + a.shape[along], axis=along))
        at += a.shape[along]
    return tuple(finished)


def from_everyone(x, axis):
    length = lax.axis_size(axis)
    return lax.all_to_all(jnp.broadcast_to(x[None], (length, *x.shape)), axis, 0, 0, tiled=True)


def of_everyone(x, axis):
    return from_everyone(x, axis).astype(jnp.float32).sum(axis=0)


def norm_apply(raw, gain):
    inverse = lax.rsqrt(jnp.mean(raw * raw, axis=-1, keepdims=True) + EPS)
    return (raw * inverse * gain, inverse)


def norm_back(raw, inverse, gain, upstream):
    weighted = upstream * gain
    return inverse * weighted - raw * inverse * inverse * inverse * jnp.mean(
        weighted * raw, axis=-1, keepdims=True
    )


def sample_grads(normed, out_heads, keys_all, values_all, tiles_here, score_scale):
    text_rows, kv_here, group_size, head_dim = normed.shape
    block_len = keys_all.shape[0] // MAX_TILES
    stat_shape = (kv_here, group_size, text_rows, 1)

    def scores_of(block_at):
        key_block = keys_all[block_at * block_len : (block_at + 1) * block_len]
        return (
            jnp.einsum("tkgd,jkd->kgtj", normed, key_block, preferred_element_type=jnp.float32)
            * score_scale
        )

    row_max = jnp.full(stat_shape, NEG, jnp.float32)
    row_sum = jnp.zeros(stat_shape, jnp.float32)
    for block_at in range(MAX_TILES):
        live_flag = block_at < tiles_here

        def update_stats(carry, block_at=block_at, live_flag=live_flag):
            old_max, old_sum = carry
            scores = jnp.where(live_flag, scores_of(block_at), NEG)
            new_max = jnp.maximum(old_max, jnp.max(scores, axis=-1, keepdims=True))
            new_sum = old_sum * jnp.exp(old_max - new_max) + jnp.sum(
                jnp.exp(scores - new_max), axis=-1, keepdims=True
            )
            return (new_max, new_sum)

        row_max, row_sum = update_stats((row_max, row_sum))

    def probs_of(block_at, live_flag):
        scores = scores_of(block_at)
        return jnp.where(live_flag, jnp.exp(scores - row_max) / row_sum, 0.0)

    attn_total = jnp.zeros((text_rows, kv_here, group_size, head_dim), jnp.float32)
    value_part = jnp.zeros((keys_all.shape[0], kv_here, head_dim), jnp.float32)
    for block_at in range(MAX_TILES):
        live_flag = block_at < tiles_here

        def forward_block(carry, block_at=block_at, live_flag=live_flag):
            attn_now, value_now = carry
            probs_b = probs_of(block_at, live_flag).astype(jnp.bfloat16)
            value_block = values_all[block_at * block_len : (block_at + 1) * block_len]
            attn_now = attn_now + jnp.einsum(
                "kgtj,jkd->tkgd", probs_b, value_block, preferred_element_type=jnp.float32
            )
            block_grad = jnp.einsum(
                "kgtj,tkgd->jkd", probs_b, out_heads, preferred_element_type=jnp.float32
            )
            value_now = value_now.at[block_at * block_len : (block_at + 1) * block_len].set(
                block_grad
            )
            return (attn_now, value_now)

        attn_total, value_part = forward_block((attn_total, value_part))
    attn_b = attn_total.astype(jnp.bfloat16)
    delta = jnp.sum(out_heads.astype(jnp.float32) * attn_b.astype(jnp.float32), axis=-1)
    delta = delta.transpose(1, 2, 0)[..., None]
    dnormed = jnp.zeros((text_rows, kv_here, group_size, head_dim), jnp.float32)
    key_part = jnp.zeros((keys_all.shape[0], kv_here, head_dim), jnp.float32)
    for block_at in range(MAX_TILES):
        live_flag = block_at < tiles_here

        def backward_block(carry, block_at=block_at, live_flag=live_flag):
            query_now, key_now = carry
            probs = probs_of(block_at, live_flag)
            key_block = keys_all[block_at * block_len : (block_at + 1) * block_len]
            value_block = values_all[block_at * block_len : (block_at + 1) * block_len]
            dprobs = jnp.einsum(
                "tkgd,jkd->kgtj", out_heads, value_block, preferred_element_type=jnp.float32
            )
            dscores = (probs * (dprobs - delta)).astype(jnp.bfloat16)
            query_now = query_now + jnp.einsum(
                "kgtj,jkd->tkgd", dscores, key_block, preferred_element_type=jnp.float32
            )
            block_grad = (
                jnp.einsum("kgtj,tkgd->jkd", dscores, normed, preferred_element_type=jnp.float32)
                * score_scale
            )
            key_now = key_now.at[block_at * block_len : (block_at + 1) * block_len].set(block_grad)
            return (query_now, key_now)

        dnormed, key_part = backward_block((dnormed, key_part))
    return (dnormed * score_scale, key_part, value_part)


def local(queries, vision, key_weight, value_weight, query_gain, key_gain, out_grad, tile_count):
    head_dim = query_gain.shape[0]
    samples_here, vision_rows, model_width = vision.shape
    text_rows = queries.shape[1]
    kv_here = key_weight.shape[1] // head_dim
    group_size = queries.shape[2] // head_dim // kv_here
    score_scale = head_dim ** (-0.5)
    flat_vision = vision.reshape(samples_here * vision_rows, model_width)
    key_raw = jnp.dot(flat_vision, key_weight, preferred_element_type=jnp.float32)
    key_raw = key_raw.reshape(samples_here, vision_rows, kv_here, head_dim)
    key_normed, key_inverse = norm_apply(key_raw, key_gain)
    own_keys = key_normed.astype(jnp.bfloat16)
    own_values = jnp.dot(flat_vision, value_weight, preferred_element_type=jnp.float32).astype(
        jnp.bfloat16
    )
    own_values = own_values.reshape(samples_here, vision_rows, kv_here, head_dim)
    keys_all, values_all = in_one_piece((own_keys, own_values), "seq", 1, 0)
    query_raw = queries.astype(jnp.float32).reshape(
        samples_here, text_rows, kv_here, group_size, head_dim
    )
    query_normed, query_inverse = norm_apply(query_raw, query_gain)
    normed = query_normed.astype(jnp.bfloat16)
    out_heads = out_grad.reshape(samples_here, text_rows, kv_here, group_size, head_dim)
    query_list = []
    key_list = []
    value_list = []
    for sample_at in range(samples_here):
        query_part, key_part, value_part = sample_grads(
            normed[sample_at],
            out_heads[sample_at],
            keys_all[sample_at],
            values_all[sample_at],
            tile_count[sample_at],
            score_scale,
        )
        query_list.append(query_part)
        key_list.append(key_part)
        value_list.append(value_part)
    key_sum, value_sum = in_one_piece_2(
        (jnp.stack(key_list).astype(jnp.bfloat16), jnp.stack(value_list).astype(jnp.bfloat16)),
        "seq",
        1,
        0,
    )
    key_grad = norm_back(key_raw, key_inverse, key_gain, key_sum).astype(jnp.bfloat16)
    value_grad = value_sum.astype(jnp.bfloat16)
    query_grad = norm_back(query_raw, query_inverse, query_gain, jnp.stack(query_list))
    query_grad = query_grad.astype(jnp.bfloat16).reshape(queries.shape)
    key_flat = key_grad.reshape(samples_here * vision_rows, kv_here * head_dim)
    value_flat = value_grad.reshape(samples_here * vision_rows, kv_here * head_dim)
    heads_key, heads_value = in_one_piece((key_grad, value_grad), "mp", 2, 0)
    rows_key, rows_value = (
        lax.all_to_all(key_weight, "mp", split_axis=0, concat_axis=1, tiled=True),
        lax.all_to_all(value_weight, "mp", split_axis=0, concat_axis=1, tiled=True),
    )
    every_head = heads_key.shape[2] * head_dim
    vision_part = jnp.einsum(
        "rc,dc->rd",
        heads_key.reshape(samples_here * vision_rows, every_head),
        rows_key,
        preferred_element_type=jnp.float32,
    )
    vision_part = vision_part + jnp.einsum(
        "rc,dc->rd",
        heads_value.reshape(samples_here * vision_rows, every_head),
        rows_value,
        preferred_element_type=jnp.float32,
    )
    vision_grad = vision_part.astype(jnp.bfloat16).reshape(
        samples_here, vision_rows, vision_part.shape[1]
    )
    key_weight_local = jnp.einsum(
        "rd,rc->dc", flat_vision, key_flat, preferred_element_type=jnp.float32
    )
    value_weight_local = jnp.einsum(
        "rd,rc->dc", flat_vision, value_flat, preferred_element_type=jnp.float32
    )
    key_shard, value_shard = tuple(
        (
            part.astype(jnp.float32)
            for part in in_one_piece_3(
                (key_weight_local.astype(jnp.bfloat16), value_weight_local.astype(jnp.bfloat16)),
                "seq",
                0,
                1,
            )
        )
    )
    key_shard, value_shard = (
        of_everyone(key_shard.astype(jnp.bfloat16), "dp").astype(jnp.float32),
        of_everyone(value_shard.astype(jnp.bfloat16), "dp").astype(jnp.float32),
    )
    key_weight_grad, value_weight_grad = tuple(
        (
            part.astype(jnp.float32)
            for part in in_one_piece(
                (key_shard.astype(jnp.bfloat16), value_shard.astype(jnp.bfloat16)), "seq", 0, 1
            )
        )
    )
    return (query_grad, vision_grad, key_weight_grad, value_weight_grad)


def solution(mesh):
    in_specs = (
        P("dp", "seq", "mp"),
        P("dp", "seq", None),
        P(None, "mp"),
        P(None, "mp"),
        P(),
        P(),
        P("dp", "seq", "mp"),
        P("dp"),
    )
    out_specs = (P("dp", "seq", "mp"), P("dp", "seq", "mp"), P(None, "mp"), P(None, "mp"))
    return jax.shard_map(local, mesh=mesh, in_specs=in_specs, out_specs=out_specs, check_vma=False)
```

profile of v0, /device:TPU:1, one launch (start us, length us, event | category | flops | bytes accessed | tf_op | source)
XLA Modules:
  0.0 306.4 jit_solution(3572372430271718063)
XLA Ops:
  7.2 1.3 copy-done
  8.5 1.7 convolution_convert_fusion
  10.3 1.9 multiply_reduce_fusion.2
  19.8 55.8 %all-gather.3.cloned.1.call-done = bf16[4,1280,1,128]{3,1,2,0:T(8,128)(2,1)} async-done(((bf16[4,80,1,128]{3,1,2,0:T(8,128)(2,1)}), bf16[4,1280,1,128]{3,1,2,0:T(8,128)(2,1)}) %all-gather.3.cloned.1.call-update) | async-done | bytes 1310736 | tf_op jit(solution)/shard_map/all_gather | solution.py:19
  75.5 1.3 select_reduce_fusion.2
  76.8 1.2 select_reduce_fusion.1
  92.4 26.5 %all_to_all.53 = bf16[16,4,80,1,128]{4,2,3,1,0:T(8,128)(2,1)S(1)} all-to-all(bf16[16,4,80,1,128]{4,2,3,1,0:T(8,128)(2,1)S(1)} %maximum_bitcast_fusion), channel_id=1, replica_groups=mesh['dp'=2,'seq'=16,'mp'=8] {'seq'}, dimensions={0} | all-to-all | bytes 2621440 | tf_op jit(solution)/shard_map/all_to_all | solution.py:29
  120.3 1.5 pad_maximum_fusion
  121.9 7.7 %all-to-all-start.2 = ((bf16[8,512,128]{2,1,0:T(8,128)(2,1)}), bf16[8,512,128]{2,1,0:T(8,128)(2,1)S(1)}, u32[]{:S(2)}, u32[]{:S(2)}) async-start(bf16[8,512,128]{2,1,0:T(8,128)(2,1)} %bitcast.234), calls=%async_computation.2 | async-start | bytes 2097152 | tf_op jit(solution)/shard_map/all_to_all | solution.py:209
  129.5 69.5 %reduce-scatter.2.cloned.1.call-done = bf16[256,256]{0,1:T(8,128)(2,1)} async-done(((bf16[4096,256]{0,1:T(8,128)(2,1)}), bf16[256,256]{0,1:T(8,128)(2,1)}) %reduce-scatter.2.cloned.1.call-update) | async-done | bytes 131088 | tf_op jit(solution)/shard_map/reduce_scatter | solution.py:44
  199.0 0.9 fusion.141
  200.8 14.1 %all_to_all.54 = bf16[2,256,128]{2,1,0:T(8,128)(2,1)S(1)} all-to-all(bf16[2,256,128]{2,1,0:T(8,128)(2,1)S(1)} %broadcast_in_dim.35), channel_id=1, replica_groups=mesh['dp'=2,'seq'=16,'mp'=8] {'dp'}, dimensions={0} | all-to-all | bytes 262144 | tf_op jit(solution)/shard_map/all_to_all | solution.py:53
  215.8 3.8 %all_to_all.55 = bf16[2,256,128]{2,1,0:T(8,128)(2,1)S(1)} all-to-all(bf16[2,256,128]{2,1,0:T(8,128)(2,1)S(1)} %broadcast_in_dim.70), channel_id=1, replica_groups=mesh['dp'=2,'seq'=16,'mp'=8] {'dp'}, dimensions={0} | all-to-all | bytes 262144 | tf_op jit(solution)/shard_map/all_to_all | solution.py:53
  219.6 5.7 %all-to-all-start.1 = ((bf16[8,512,128]{2,1,0:T(8,128)(2,1)}), bf16[8,512,128]{2,1,0:T(8,128)(2,1)}, u32[]{:S(2)}, u32[]{:S(2)}) async-start(bf16[8,512,128]{2,1,0:T(8,128)(2,1)} %bitcast.231), calls=%async_computation.1 | async-start | bytes 2097152 | tf_op jit(solution)/shard_map/all_to_all | solution.py:208
  226.2 1.5 copy.190
  227.7 12.4 %all-to-all-done.1 = bf16[8,512,128]{2,1,0:T(8,128)(2,1)} async-done(((bf16[8,512,128]{2,1,0:T(8,128)(2,1)}), bf16[8,512,128]{2,1,0:T(8,128)(2,1)}, u32[]{:S(2)}, u32[]{:S(2)}) %all-to-all-start.1) | async-done | bytes 1048608 | tf_op jit(solution)/shard_map/all_to_all | solution.py:208
  240.0 2.3 copy.188
  242.3 1.4 fusion.132
  243.7 1.4 convolution_add_fusion.3
  245.1 1.2 convolution_add_fusion.2
  246.3 1.2 fusion.44
  248.4 1.4 fusion.131
  249.8 1.4 convolution_add_fusion.9
  251.2 1.2 convolution_add_fusion.8
  252.4 1.9 fusion.45
  254.4 1.8 copy.163
  256.2 1.2 fusion.91
  257.4 1.2 fusion.88
  259.4 34.0 %all_gather.10 = bf16[4,80,8,128]{3,1,0,2:T(8,128)(2,1)S(1)} all-gather(bf16[4,80,1,128]{3,1,0,2:T(8,128)(2,1)S(1)} %pad_maximum_fusion.3), channel_id=1, replica_groups=mesh['dp'=2,'seq'=16,'mp'=8] {'mp'}, dimensions={2}, use_global_device_ids=true | all-gather | bytes 737280 | tf_op jit(solution)/shard_map/all_gather | solution.py:19
  293.7 0.9 copy-done.2
  295.0 1.0 fusion.46
  296.0 3.8 %slice_convert_fusion = (f32[4096,128]{1,0:T(8,128)}, f32[4096,128]{1,0:T(8,128)}) fusion(bf16[4096,256]{1,0:T(8,128)(2,1)} %all-gather.5.cloned.1.call-done), kind=kLoop, calls=%fused_computation.142 | loop fusion | flops 1048576 | bytes 6291456 | tf_op jit(solution)/shard_map/convert_element_type | solution.py:250
  (136 shorter events, 22.7 us)
Async XLA Ops:
  7.2 1.3 copy-start
  7.2 68.4 %all-gather.3.cloned.1.call-start = ((), (), s32[]{:S(2)}) async-start(), calls=%async_computation.6 | async-start | bytes 1392640 | tf_op jit(solution)/shard_map/all_gather | solution.py:19
  10.2 2.0 copy-start.18
  10.2 2.8 copy-start.20
  10.2 8.6 %copy-start.16 = (bf16[2,128,512]{2,1,0:T(8,128)(2,1)S(1)}, bf16[2,128,512]{2,1,0:T(8,128)(2,1)}, u32[]{:S(2)}) copy-start(bf16[2,128,512]{2,1,0:T(8,128)(2,1)} %param.40) | copy-start | bytes 786436
  10.2 8.8 %copy-start.17 = (bf16[2,128,512]{2,1,0:T(8,128)(2,1)S(1)}, bf16[2,128,512]{2,1,0:T(8,128)(2,1)}, u32[]{:S(2)}) copy-start(bf16[2,128,512]{2,1,0:T(8,128)(2,1)} %param.46) | copy-start | bytes 786436
  13.0 186.0 %reduce-scatter.2.cloned.1.call-start = ((), (), s32[]{:S(2)}) async-start(), calls=%async_computation.7 | async-start | bytes 2228224 | tf_op jit(solution)/shard_map/reduce_scatter | solution.py:44
  18.8 0.7 copy-start.19
  75.5 2.4 copy-start.3
  81.6 0.7 copy-start.14
  86.7 0.7 copy-start.15
  88.0 0.7 copy-start.4
  88.8 0.7 copy-start.5
  89.5 0.7 copy-start.7
  90.2 0.7 copy-start.9
  91.0 0.7 copy-start.10
  91.7 0.7 copy-start.12
  121.9 78.9 %all-to-all-start.2 = ((bf16[8,512,128]{2,1,0:T(8,128)(2,1)}), bf16[8,512,128]{2,1,0:T(8,128)(2,1)S(1)}, u32[]{:S(2)}, u32[]{:S(2)}) async-start(bf16[8,512,128]{2,1,0:T(8,128)(2,1)} %bitcast.234), calls=%async_computation.2 | async-start | bytes 2097152 | tf_op jit(solution)/shard_map/all_to_all | solution.py:209
  200.8 18.8 %copy-start.1 = (bf16[8,512,128]{2,1,0:T(8,128)(2,1)}, bf16[8,512,128]{2,1,0:T(8,128)(2,1)S(1)}, u32[]{:S(2)}) copy-start(bf16[8,512,128]{2,1,0:T(8,128)(2,1)S(1)} %all-to-all-done.2) | copy-start | bytes 3145732
  219.6 20.4 %all-to-all-start.1 = ((bf16[8,512,128]{2,1,0:T(8,128)(2,1)}), bf16[8,512,128]{2,1,0:T(8,128)(2,1)}, u32[]{:S(2)}, u32[]{:S(2)}) async-start(bf16[8,512,128]{2,1,0:T(8,128)(2,1)} %bitcast.231), calls=%async_computation.1 | async-start | bytes 2097152 | tf_op jit(solution)/shard_map/all_to_all | solution.py:208
  225.4 70.6 %all-gather.5.cloned.1.call-start = ((), (), s32[]{:S(2)}) async-start(), calls=%async_computation.8 | async-start | bytes 2228224 | tf_op jit(solution)/shard_map/all_gather | solution.py:19
  242.3 2.8 copy-start.6
  242.3 4.0 %copy-start.8 = (bf16[4,128,320]{1,2,0:T(8,128)(2,1)S(1)}, bf16[4,128,320]{1,2,0:T(8,128)(2,1)}, u32[]{:S(2)}) copy-start(bf16[4,128,320]{1,2,0:T(8,128)(2,1)} %copy-done.7) | copy-start | bytes 983044
  248.4 2.8 copy-start.11
  248.4 4.0 %copy-start.13 = (bf16[4,128,320]{1,2,0:T(8,128)(2,1)S(1)}, bf16[4,128,320]{1,2,0:T(8,128)(2,1)}, u32[]{:S(2)}) copy-start(bf16[4,128,320]{1,2,0:T(8,128)(2,1)} %copy-done.12) | copy-start | bytes 983044
  293.4 1.2 copy-start.2
Sparse Core Ops, SparseCore 0:
  13.1 62.3 all-gather.2
  122.0 77.0 reduce-scatter.1
  228.0 65.5 all-gather.4
where the time goes:
time: 313 us; the launch traced here: 306 us
  waiting for transfers between devices  138 us (44%)
  blocking collectives  78.5 us (25%)
  matrix products  29.6 us (9%)
  between operations  19.6 us (6%)
  local copies, waits for them, and re-layouts  16.4 us (5%)
  starting transfers between devices  13.5 us (4%)
  other arithmetic  11.1 us (4%)
    reduce_scatter x1, waiting for transfers between devices, in_one_piece_3(): lax.psum_scatter(both, axis, scatter_dimension=dim, tiled=True)  69.5 us
    all_gather x2, waiting for transfers between devices, in_one_piece(): lax.all_gather(both, axis, axis=dim, tiled=True)  55.8 us
    all_gather x1, blocking collectives, in_one_piece(): lax.all_gather(both, axis, axis=dim, tiled=True)  34 us
    all_to_all x1, blocking collectives, sum_at_owner(): pieces = lax.all_to_all(cut_along(x, dim, length), axis, 0, 0, tiled=True)  26.5 us
    all_to_all x2, blocking collectives, from_everyone(): lax.all_to_all(jnp.broadcast_to(x[None], (length, *x.shape)), axis, 0, 0,...  18 us
    all_to_all x1, waiting for transfers between devices, local(): lax.all_to_all(key_weight, 'mp', split_axis=0, concat_axis=1, tiled=True)  12.4 us
    dot_general x8, matrix products, backward_block(): jnp.einsum('kgtj,jkd->tkgd', dscores, key_block, preferred_element_type=j...  11.2 us
    all_to_all x1, starting transfers between devices, local(): lax.all_to_all(value_weight, 'mp', split_axis=0, concat_axis=1, tiled=True)  7.67 us
  transfers between devices with their start and end apart: 5, of which 3 were waited for; matrix products, arithmetic and copies ran while one was open for 9% of the time, Pallas kernels for 0%

commit v1 on v0

v1 whole, which is shorter than its diff:
```python
import functools

import jax
import jax.numpy as jnp
from jax import lax
from jax.experimental import pallas as pl
from jax.experimental.pallas import tpu as pltpu
from jax.sharding import PartitionSpec as P

EPS = 1e-05
NEG = -1e30
LOG2E = 1.4426950408889634
MESH = pl.DeviceIdType.MESH
NT = (((1,), (1,)), ((), ()))
TN = (((0,), (0,)), ((), ()))
F32 = jnp.float32
BF16 = jnp.bfloat16
N_COPY = 300

SEQ_A = ((0, 1, 4), (0, -1, 3), (1, 1, 3), (1, -1, 4))
SEQ_B = ((0, 1, 4), (0, -1, 3))
MP_A = ((0, 1, 2), (0, -1, 1), (1, 1, 1), (1, -1, 2))


def dot(a, b, dims=None):
    if dims is None:
        return jnp.dot(a, b, preferred_element_type=F32)
    return lax.dot_general(a, b, dims, preferred_element_type=F32)


class Copies:
    def __init__(self, send_sems, recv_sems):
        self.send_sems, self.recv_sems, self.all = send_sems, recv_sems, []

    def start(self, src, dst, device):
        at = len(self.all)
        copy = pltpu.make_async_remote_copy(
            src_ref=src,
            dst_ref=dst,
            send_sem=self.send_sems.at[at],
            recv_sem=self.recv_sems.at[at],
            device_id=device,
            device_id_type=MESH,
        )
        copy.start()
        self.all.append(copy)
        return copy

    def drain(self):
        for copy in self.all:
            copy.wait_send()


class Slots:
    def __init__(self, copies, stage, land):
        self.copies, self.stage, self.land, self.used = copies, stage, land, 0

    def send(self, value, device):
        at = self.used
        self.used += 1
        self.stage[at] = value.astype(BF16)
        copy = self.copies.start(self.stage.at[at], self.land.at[at], device)
        return copy, at

    def take(self, pending):
        copy, at = pending
        copy.wait_recv()
        return self.land[at].astype(F32)


def gather_a(copies, chunk, ring, across, hook):
    side = copies.start(chunk(0, 0), chunk(0, 0), across)
    pend = {}
    for i in (0, 1):
        pend[i] = copies.start(chunk(0, 0), chunk(0, 0), ring[SEQ_A[i][1]])
    hook(0, 0)
    yield
    side.wait_recv()
    for i in (2, 3):
        pend[i] = copies.start(chunk(0, 1), chunk(0, 1), ring[SEQ_A[i][1]])
    hook(0, 1)
    yield
    for t in range(1, 5):
        for i, (col, way, hops) in enumerate(SEQ_A):
            if t <= hops:
                pend[i].wait_recv()
                here = chunk(-way * t, col)
                if t < hops:
                    pend[i] = copies.start(here, here, ring[way])
                hook(-way * t, col)
        yield


def gather_b(copies, chunk, ring, across, hook):
    pend = {}
    for i in (0, 1):
        pend[i] = copies.start(chunk(0, 0), chunk(0, 0), ring[SEQ_B[i][1]])
    sides = [(0, copies.start(chunk(0, 0), chunk(0, 0), across))]
    hook(0, 0)
    yield
    for t in range(1, 5):
        for i, (col, way, hops) in enumerate(SEQ_B):
            if t <= hops:
                pend[i].wait_recv()
                here = chunk(-way * t, col)
                if t < hops:
                    pend[i] = copies.start(here, here, ring[way])
                sides.append((-way * t, copies.start(here, here, across)))
                hook(-way * t, col)
        yield
    for at, side in sides:
        side.wait_recv()
        hook(at, 1)


def scatter_a(slots, own, ring, across, streams, finish):
    pend = {}
    most = max(hops for _, _, hops in streams)
    for t in range(most):
        for i, (col, way, hops) in enumerate(streams):
            if t < hops:
                value = own(way * (hops - t), col)
                if t > 0:
                    value = value + slots.take(pend[i])
                pend[i] = slots.send(value, ring[way])
        yield
    value = own(0, 1)
    for i in (2, 3):
        value = value + slots.take(pend[i])
    side = slots.send(value, across)
    yield
    value = own(0, 0)
    for i in (0, 1):
        value = value + slots.take(pend[i])
    finish(value + slots.take(side))


def scatter_b(slots, own, ring, across, finish):
    sides = {}
    for at in (4, -3, 3, -2, 2, -1, 1, 0):
        sides[at] = slots.send(own(at, 1), across)
    yield
    pend = {}
    for t in range(4):
        for i, (_, way, hops) in enumerate(SEQ_B):
            if t < hops:
                at = way * (hops - t)
                value = own(at, 0) + slots.take(sides[at])
                if t > 0:
                    value = value + slots.take(pend[i])
                pend[i] = slots.send(value, ring[way])
        yield
    value = own(0, 0) + slots.take(sides[0])
    for i in (0, 1):
        value = value + slots.take(pend[i])
    finish(value)


def step(generators):
    alive = []
    for generator in generators:
        try:
            next(generator)
            alive.append(generator)
        except StopIteration:
            pass
    return alive


def kernel(
    sizes,
    q_hbm, vis_hbm, wk_hbm, wv_hbm, qgain_ref, kgain_ref, do_hbm, tiles_ref,
    qgrad, vgrad, wgk, wgv,
    vis, visw, w, q2, do2, qn, dot_t, kraw, kall, vall, s_ref, dk, dv, ksum, vsum,
    kvg, kvgp, wgt, stage_d, land_d, stage_e, land_e, stage_c, land_c,
    send_sems, recv_sems, in_sems,
):
    nz, ny = sizes
    samples, rows, tile = 2, 80, 320
    n_seq = 2 * nz
    heads = 4
    text = q_hbm.shape[1]
    width = vis_hbm.shape[1]
    half = width // 2
    slab = half // n_seq
    share = vgrad.shape[1]
    head_dim = 128
    score_scale = head_dim ** (-0.5)

    core = lax.axis_index("dp")
    seq = lax.axis_index("seq")
    mp = lax.axis_index("mp")
    z, col = seq // 2, lax.rem(seq, 2)
    xh, y = mp // ny, lax.rem(mp, ny)
    sign = 1 - 2 * core

    def z_at(k):
        return lax.rem(z + sign * k + 2 * nz, nz)

    def y_at(k):
        return lax.rem(y + k + 2 * ny, ny)

    ring = {k: {"seq": z_at(k) * 2 + col} for k in (1, -1)}
    across = {"seq": z * 2 + 1 - col}
    partner = {"dp": 1 - core}
    y_ring = {k: {"mp": xh * ny + y_at(k)} for k in (1, -1)}
    y_across = {"mp": (1 - xh) * ny + y}
    peers = (ring[1], ring[-1], across, partner, y_ring[1], y_ring[-1], y_across)

    local = []

    def load(src, dst):
        copy = pltpu.make_async_copy(src, dst, in_sems.at[len(local)])
        copy.start()
        local.append(copy)
        return copy

    parts = 4
    piece = width // parts
    loads = []
    for p in range(parts):
        cols = pl.ds(p * piece, piece)
        loads.append(
            (
                load(vis_hbm.at[:, cols], vis.at[:, cols]),
                load(wk_hbm.at[cols, :], w.at[cols, pl.ds(0, 128)]),
                load(wv_hbm.at[cols, :], w.at[cols, pl.ds(128, 128)]),
            )
        )
    q_loads = []
    for a in range(samples):
        for h in range(heads):
            here = pl.ds(h * text, text)
            q_loads.append(load(q_hbm.at[a, :, pl.ds(h * 128, 128)], q2.at[a, here, :]))
            q_loads.append(load(do_hbm.at[a, :, pl.ds(h * 128, 128)], do2.at[a, here, :]))
    mine = pl.ds(pl.multiple_of(core * half, 128), half)
    theirs = pl.ds(pl.multiple_of((1 - core) * half, 128), half)
    own_half = load(vis_hbm.at[:, mine], visw.at[pl.ds(0, samples * rows), :])

    barrier = pltpu.get_barrier_semaphore()
    for peer in peers:
        pl.semaphore_signal(barrier, inc=1, device_id=peer, device_id_type=MESH)

    total = jnp.zeros((samples * rows, 256), F32)
    for p in range(parts):
        for copy in loads[p]:
            copy.wait()
        total = total + dot(vis[:, p * piece : (p + 1) * piece], w[p * piece : (p + 1) * piece, :])
    key_raw = total[:, :128]
    kraw[...] = key_raw
    key_inverse = lax.rsqrt(jnp.mean(key_raw * key_raw, axis=-1, keepdims=True) + EPS)
    keys = (key_raw * key_inverse * kgain_ref[...]).astype(BF16)
    values = total[:, 128:].astype(BF16)
    own_rows = pl.ds(pl.multiple_of(seq * rows, 16), rows)
    for a in range(samples):
        kall[a, own_rows, :] = keys[a * rows : (a + 1) * rows]
        vall[a, own_rows, :] = values[a * rows : (a + 1) * rows]

    pl.semaphore_wait(barrier, len(peers))
    copies = Copies(send_sems, recv_sems)

    def owner(k, other):
        return z_at(k) * 2 + (1 - col if other else col)

    def no_hook(k, other):
        del k, other

    def key_chunk(ref, a):
        def chunk(k, other):
            return ref.at[a, pl.ds(pl.multiple_of(owner(k, other) * rows, 16), rows), :]

        return chunk

    first = [
        gather_a(copies, key_chunk(kall, 0), ring, across, no_hook),
        gather_b(copies, key_chunk(vall, 0), ring, across, no_hook),
    ]
    second = [
        gather_a(copies, key_chunk(kall, 1), ring, across, no_hook),
        gather_b(copies, key_chunk(vall, 1), ring, across, no_hook),
    ]

    def prepare(a):
        raw = q2[a].astype(F32)
        inverse = lax.rsqrt(jnp.mean(raw * raw, axis=-1, keepdims=True) + EPS)
        qn[a] = (raw * inverse * qgain_ref[...]).astype(BF16)
        for h in range(heads):
            block = do2[a, pl.ds(h * text, text), :].astype(F32)
            dot_t[a, :, pl.ds(h * text, text)] = block.T

    first = step(first)
    second = step(second)
    vision_swap = copies.start(
        vis_hbm.at[:, theirs], visw.at[pl.ds(samples * rows, samples * rows), :], partner
    )
    for copy in q_loads:
        copy.wait()
    prepare(0)
    first = step(first)
    second = step(second)
    prepare(1)
    while first:
        first = step(first)
        second = step(second)

    n_rows = heads * text

    def scores_pass(a):
        def body(k, row_max):
            at = pl.ds(pl.multiple_of(k * tile, tile), tile)
            s = dot(kall[a, at, :], qn[a], NT)
            s = s + jnp.where(k < tiles_ref[a], 0.0, NEG)
            s_ref[at, :] = s
            return jnp.maximum(row_max, jnp.max(s, axis=0, keepdims=True))

        return lax.fori_loop(0, 4, body, jnp.full((1, n_rows), NEG, F32))

    def exp_pass(row_max):
        def body(k, row_sum):
            at = pl.ds(pl.multiple_of(k * tile, tile), tile)
            e = jnp.exp2((s_ref[at, :] - row_max) * (score_scale * LOG2E))
            s_ref[at, :] = e
            return row_sum + jnp.sum(e, axis=0, keepdims=True)

        return 1.0 / lax.fori_loop(0, 4, body, jnp.zeros((1, n_rows), F32))

    def value_pass(a, inverse_sum):
        def body(k, attn):
            at = pl.ds(pl.multiple_of(k * tile, tile), tile)
            probs_b = (s_ref[at, :] * inverse_sum).astype(BF16)
            dv[a, at, :] = dot(probs_b, do2[a])
            return attn + dot(vall[a, at, :], probs_b, TN)

        attn = lax.fori_loop(0, 4, body, jnp.zeros((head_dim, n_rows), F32))
        return jnp.sum(dot_t[a] * attn.astype(BF16).astype(F32), axis=0, keepdims=True)

    def key_pass(a, inverse_sum, delta):
        def body(k, dn):
            at = pl.ds(pl.multiple_of(k * tile, tile), tile)
            dprobs = dot(vall[a, at, :], do2[a], NT)
            ds = (s_ref[at, :] * inverse_sum * (dprobs - delta)).astype(BF16)
            dk[a, at, :] = dot(ds, qn[a]) * score_scale
            return dn + dot(kall[a, at, :], ds, TN)

        return lax.fori_loop(0, 4, body, jnp.zeros((head_dim, n_rows), F32))

    def query_pass(a, dn):
        for h in range(heads):
            here = slice(h * text, (h + 1) * text)
            raw = q2[a, here, :].astype(F32)
            inverse = lax.rsqrt(jnp.mean(raw * raw, axis=-1, keepdims=True) + EPS)
            u = (dn[:, here] * score_scale).T * qgain_ref[...]
            mean = jnp.mean(u * raw, axis=-1, keepdims=True)
            grad = inverse * u - raw * (inverse * inverse * inverse) * mean
            qgrad[a, :, pl.ds(h * 128, 128)] = grad.astype(BF16)

    def own_part(ref, a):
        def own(k, other):
            return ref[a, pl.ds(pl.multiple_of(owner(k, other) * rows, 16), rows), :]

        return own

    def own_sum(ref, a):
        def finish(value):
            ref[pl.ds(a * rows, rows), :] = value

        return finish

    slots_d = Slots(copies, stage_d, land_d)

    def value_scatter(a):
        return scatter_b(slots_d, own_part(dv, a), ring, across, own_sum(vsum, a))

    def key_scatter(a):
        return scatter_a(slots_d, own_part(dk, a), ring, across, SEQ_A, own_sum(ksum, a))

    row_max = scores_pass(0)
    second = step(second)
    inverse_sum = exp_pass(row_max)
    second = step(second)
    delta = value_pass(0, inverse_sum)
    while second:
        second = step(second)
    going = step([value_scatter(0)])
    dn = key_pass(0, inverse_sum, delta)
    going = step(going + [key_scatter(0)])
    query_pass(0, dn)
    row_max = scores_pass(1)
    going = step(going)
    inverse_sum = exp_pass(row_max)
    going = step(going)
    delta = value_pass(1, inverse_sum)
    going = step(going + [value_scatter(1)])
    dn = key_pass(1, inverse_sum, delta)
    going = step(going + [key_scatter(1)])
    query_pass(1, dn)
    while going:
        going = step(going)

    raw = kraw[...]
    inverse = lax.rsqrt(jnp.mean(raw * raw, axis=-1, keepdims=True) + EPS)
    u = ksum[...] * kgain_ref[...]
    mean = jnp.mean(u * raw, axis=-1, keepdims=True)
    kvg[:, :128] = (inverse * u - raw * (inverse * inverse * inverse) * mean).astype(BF16)
    kvg[:, 128:] = vsum[...].astype(BF16)
    swap = copies.start(kvg, kvgp, partner)

    def vision_part(k, other):
        at = (1 - xh if other else xh) * ny + y_at(k)
        block = w[pl.ds(pl.multiple_of(at * share, share), share), :]
        return dot(kvg[...], block, NT)

    def vision_done(value):
        vgrad[...] = value.astype(BF16)

    slots_c = Slots(copies, stage_c, land_c)
    vision = step([scatter_a(slots_c, vision_part, y_ring, y_across, MP_A, vision_done)])

    swap.wait_recv()
    own_half.wait()
    vision_swap.wait_recv()
    own_t = kvg[...].astype(F32).T.astype(BF16)
    their_t = kvgp[...].astype(F32).T.astype(BF16)
    n_own = samples * rows
    for i in range(n_seq // 2):
        lanes = slice(i * 2 * slab, (i + 1) * 2 * slab)
        block = dot(own_t, visw[:n_own, lanes]) + dot(their_t, visw[n_own:, lanes])
        wgt[2 * i] = block[:, :slab]
        wgt[2 * i + 1] = block[:, slab:]

    def own_weight(which):
        def own(k, other):
            return wgt[owner(k, other), pl.ds(which * 128, 128), :]

        return own

    def weight_chunk(ref):
        def chunk(k, other):
            start = pl.multiple_of(core * half + owner(k, other) * slab, slab)
            return ref.at[pl.ds(start, slab), :]

        return chunk

    def weight_done(ref):
        def finish(value):
            start = pl.multiple_of(core * half + seq * slab, slab)
            ref[pl.ds(start, slab), :] = value.T.astype(BF16)

        return finish

    slots_e = Slots(copies, stage_e, land_e)
    going = [
        scatter_b(slots_e, own_weight(1), ring, across, weight_done(wgv)),
        scatter_a(slots_e, own_weight(0), ring, across, SEQ_A, weight_done(wgk)),
    ]
    for _ in range(4):
        going = step(going)
    vision = step(vision)
    while going:
        going = step(going)

    handed = []

    def hand_on(ref):
        def hook(k, other):
            here = weight_chunk(ref)(k, other)
            handed.append(copies.start(here, here, partner))

        return hook

    going = [
        gather_a(copies, weight_chunk(wgk), ring, across, hand_on(wgk)),
        gather_b(copies, weight_chunk(wgv), ring, across, hand_on(wgv)),
    ]
    for _ in range(3):
        going = step(going)
    vision = step(vision)
    while going:
        going = step(going)
    while vision:
        vision = step(vision)
    for copy in handed:
        copy.wait_recv()
    copies.drain()


def local(nz, ny, queries, vision, key_weight, value_weight, query_gain, key_gain, out_grad, tile_count):
    samples, rows, width = vision.shape
    text = queries.shape[1]
    n_seq = 2 * nz
    n_own = samples * rows
    n_vis = rows * n_seq
    n_rows = 4 * text
    half = width // 2
    slab = half // n_seq
    share = width // (2 * ny)
    hbm = pl.BlockSpec(memory_space=pl.ANY)
    vmem = pl.BlockSpec(memory_space=pltpu.VMEM)
    smem = pl.BlockSpec(memory_space=pltpu.SMEM)
    query_grad, vision_grad, wgk, wgv = pl.pallas_call(
        functools.partial(kernel, (nz, ny)),
        out_shape=(
            jax.ShapeDtypeStruct(queries.shape, BF16),
            jax.ShapeDtypeStruct((n_own, share), BF16),
            jax.ShapeDtypeStruct((width, 128), BF16),
            jax.ShapeDtypeStruct((width, 128), BF16),
        ),
        in_specs=[hbm, hbm, hbm, hbm, vmem, vmem, hbm, smem],
        out_specs=(vmem, vmem, vmem, vmem),
        scratch_shapes=[
            pltpu.VMEM((n_own, width), BF16),
            pltpu.VMEM((2 * n_own, half), BF16),
            pltpu.VMEM((width, 256), BF16),
            pltpu.VMEM((samples, n_rows, 128), BF16),
            pltpu.VMEM((samples, n_rows, 128), BF16),
            pltpu.VMEM((samples, n_rows, 128), BF16),
            pltpu.VMEM((samples, 128, n_rows), F32),
            pltpu.VMEM((n_own, 128), F32),
            pltpu.VMEM((samples, n_vis, 128), BF16),
            pltpu.VMEM((samples, n_vis, 128), BF16),
            pltpu.VMEM((n_vis, n_rows), F32),
            pltpu.VMEM((samples, n_vis, 128), F32),
            pltpu.VMEM((samples, n_vis, 128), F32),
            pltpu.VMEM((n_own, 128), F32),
            pltpu.VMEM((n_own, 128), F32),
            pltpu.VMEM((n_own, 256), BF16),
            pltpu.VMEM((n_own, 256), BF16),
            pltpu.VMEM((n_seq, 256, slab), F32),
            pltpu.VMEM((60, rows, 128), BF16),
            pltpu.VMEM((60, rows, 128), BF16),
            pltpu.VMEM((30, 128, slab), BF16),
            pltpu.VMEM((30, 128, slab), BF16),
            pltpu.VMEM((7, n_own, share), BF16),
            pltpu.VMEM((7, n_own, share), BF16),
            pltpu.SemaphoreType.DMA((N_COPY,)),
            pltpu.SemaphoreType.DMA((N_COPY,)),
            pltpu.SemaphoreType.DMA((40,)),
        ],
        compiler_params=pltpu.CompilerParams(
            collective_id=0, has_side_effects=True, vmem_limit_bytes=60 * 1024 * 1024
        ),
    )(
        queries,
        vision.reshape(n_own, width),
        key_weight,
        value_weight,
        query_gain.reshape(1, 128),
        key_gain.reshape(1, 128),
        out_grad,
        tile_count,
    )
    return (
        query_grad,
        vision_grad.reshape(samples, rows, share),
        wgk.astype(F32),
        wgv.astype(F32),
    )


def solution(mesh):
    nz = mesh.shape["seq"] // 2
    ny = mesh.shape["mp"] // 2
    in_specs = (
        P("dp", "seq", "mp"),
        P("dp", "seq", None),
        P(None, "mp"),
        P(None, "mp"),
        P(),
        P(),
        P("dp", "seq", "mp"),
        P("dp"),
    )
    out_specs = (P("dp", "seq", "mp"), P("dp", "seq", "mp"), P(None, "mp"), P(None, "mp"))
    return jax.shard_map(
        functools.partial(local, nz, ny), mesh=mesh, in_specs=in_specs, out_specs=out_specs, check_vma=False
    )
```

time: 313 us -> 113 us (0.36); the launches traced: 306 us -> 113 us
  waiting for transfers between devices: 138 us -> 0 us
  Pallas kernels: 0 us -> 107 us
  blocking collectives: 78.5 us -> 0 us
  matrix products: 29.6 us -> 0 us
  between operations: 19.6 us -> 0.65 us
  local copies, waits for them, and re-layouts: 16.4 us -> 1.38 us
  starting transfers between devices: 13.5 us -> 0 us
  other arithmetic: 11.1 us -> 4.22 us
    pallas_call x0 -> x1, Pallas kernels: none -> 107 us  [local(): pl.pallas_call(functools.partial(kernel, (nz, ny)), out_shape=(jax.ShapeD...]
    reduce_scatter x1 -> x0, waiting for transfers between devices: 69.5 us -> none  [in_one_piece_3(): lax.psum_scatter(both, axis, scatter_dimension=dim, tiled=True)]
    all_gather x2 -> x0, waiting for transfers between devices: 55.8 us -> none  [in_one_piece(): lax.all_gather(both, axis, axis=dim, tiled=True)]
    all_to_all x3 -> x0, blocking collectives: 44.5 us -> none  [the longest x1 26.5 us: sum_at_owner(): pieces = lax.all_to_all(cut_along(x, dim, length), axis, 0, 0, tiled=True)]
    all_gather x1 -> x0, blocking collectives: 34 us -> none  [in_one_piece(): lax.all_gather(both, axis, axis=dim, tiled=True)]
    dot_general x54 -> x0, matrix products: 29.6 us -> none  [the longest x8 11.2 us: backward_block(): jnp.einsum('kgtj,jkd->tkgd', dscores, key_block, preferred_element_type=j...]
    all_to_all x2 -> x0, starting transfers between devices: 13.4 us -> none  [the longest x1 7.67 us: local(): lax.all_to_all(value_weight, 'mp', split_axis=0, concat_axis=1, tiled=True)]
    all_to_all x2 -> x0, waiting for transfers between devices: 12.4 us -> none  [the longest x1 12.4 us: local(): lax.all_to_all(key_weight, 'mp', split_axis=0, concat_axis=1, tiled=True)]
  transfers between devices with their start and end apart: 5 -> 0, of which waited for: 3 -> 0; matrix products, arithmetic and copies ran while one was open for 9% -> 0% of each run, Pallas kernels for 0% -> 0%
where the time goes in v1:
time: 113 us
  Pallas kernels  107 us (95%)
  other arithmetic  4.22 us (4%)
  local copies, waits for them, and re-layouts  1.38 us (1%)
    pallas_call x1, Pallas kernels, local(): pl.pallas_call(functools.partial(kernel, (nz, ny)), out_shape=(jax.ShapeD...  107 us
    convert_element_type x1, other arithmetic, local(): wgk.astype(F32)  2.77 us

profile of v1, /device:TPU:1, one launch (start us, length us, event | category | flops | bytes accessed | tf_op | source)
XLA Modules:
  0.0 112.8 jit_solution(7513065113459451154)
XLA Ops:
  0.6 106.6 %shard_map.111 = (bf16[2,128,512]{2,1,0:T(8,128)(2,1)}, bf16[160,512]{1,0:T(8,128)(2,1)}, bf16[4096,128]{1,0:T(8,128)(2,1)}, bf16[4096,128]{1,0:T(8,128)(2,1)}) custom-call(bf16[2,128,512]{2,1,0:T(8,128)(2,1)} %q_hbm.1, bf16[160,4096]{1,0:T(8,128)(2,1)} %bitcast.4, bf16[4096,128]{1,0:T(8,128)(2,1)} %wk_hbm.1, bf16[4096,128]{1,0:T(8,128)(2,1)} %wv_hbm.1, ...), custom_call_target="tpu_custom_call" | custom-call | tf_op jit(solution)/shard_map/pallas_call | solution.py:500
  107.2 0.0 copy-start
  107.2 2.8 %convert_element_type.6 = f32[4096,128]{1,0:T(8,128)} convert(bf16[4096,128]{1,0:T(8,128)(2,1)} %get-tuple-element.10) | non-fusion elementwise | flops 524288 | bytes 3145728 | tf_op jit(solution)/shard_map/convert_element_type | solution.py:555
  110.0 0.0 copy-done
  110.0 0.0 copy-start.1
  110.0 0.0 copy-start.2
  110.0 1.5 %convert_element_type.7 = f32[4096,128]{1,0:T(8,128)} convert(bf16[4096,128]{1,0:T(8,128)(2,1)S(1)} %copy-done) | non-fusion elementwise | flops 524288 | bytes 3145728 | tf_op jit(solution)/shard_map/convert_element_type | solution.py:556
  111.5 0.0 copy-done.1
  111.5 0.7 copy.14
  112.2 0.0 copy-done.2
  112.2 0.7 copy.15
Async XLA Ops:
  107.2 2.8 %copy-start = (bf16[4096,128]{1,0:T(8,128)(2,1)S(1)}, bf16[4096,128]{1,0:T(8,128)(2,1)}, u32[]{:S(2)}) copy-start(bf16[4096,128]{1,0:T(8,128)(2,1)} %get-tuple-element.11) | copy-start | bytes 3145732
  110.0 1.5 %copy-start.1 = (bf16[2,128,512]{2,1,0:T(8,128)(2,1)S(1)}, bf16[2,128,512]{2,1,0:T(8,128)(2,1)}, u32[]{:S(2)}) copy-start(bf16[2,128,512]{2,1,0:T(8,128)(2,1)} %get-tuple-element.16) | copy-start | bytes 786436
  110.0 2.2 %copy-start.2 = (bf16[160,512]{1,0:T(8,128)(2,1)S(1)}, bf16[160,512]{1,0:T(8,128)(2,1)}, u32[]{:S(2)}) copy-start(bf16[160,512]{1,0:T(8,128)(2,1)} %get-tuple-element.9) | copy-start | bytes 491524
